TPU v7x, 32 devices: a whole 2x2x4 slice. The times are simulated.
32 devices in a mesh: section: 4 (over y, x), tensor: 2 (over core), dp: 4 (over z).
Axes of the slice: x: 2, y: 2, z: 4, core: 2. Of those that a mesh axis runs over, the one named last changes fastest.
Arguments:
- hidden_in: bfloat16 [128, 4096], P('dp', 'tensor'), may hold values from -6 to 6
- norm_gain: float32 [4, 4096], P('section'), may hold values from 0.25 to 1.75
- gate_weight: bfloat16 [4, 4096, 8192], P('section', 'dp', 'tensor'), may hold values from -0.09375 to 0.09375
- up_weight: bfloat16 [4, 4096, 8192], P('section', 'dp', 'tensor'), may hold values from -0.09375 to 0.09375
- down_weight: bfloat16 [4, 4096, 8192], P('section', 'dp', 'tensor'), may hold values from -0.0625 to 0.0625
- lengths: int32 [16], P('dp'), may hold values from 3 to 8
Outputs:
- rdm: float32 [4, 16, 16], P('section', 'dp')
Inputs may be any that keep to these rules, and one draw needn't show every extreme that they name: `lengths`: the number of leading valid token rows of each sentence.
All inputs are finite; a program needn't handle non-finite values.
Results may differ from a plain program's by a relative error of at most 0.0012.
Values may be sent and summed in bfloat16 or wider, within the bound.
A program may use at most 192 MiB of HBM per device.

v0:
```python
import jax
import jax.numpy as jnp
from jax import lax
from jax.sharding import PartitionSpec as P

D = 4096
LEN = 8
MICRO = 2
SENT_DEV = 4
SENT_MB = 2
MB_TOK = 16


RMS_EPS = 1e-05
UNIT_FLOOR = 0.1
CONTRACT_LAST = (((1,), (1,)), ((), ()))


def passed_along(array, axis, by):
    peers = lax.axis_size(axis)
    pairs = [(i, i + by) for i in range(peers) if 0 <= i + by < peers]
    return lax.ppermute(array, axis, pairs)


def pool_rows(values, sentence_len):
    shaped = values.astype(jnp.float32).reshape(SENT_MB, LEN, values.shape[1])
    positions = jnp.arange(LEN, dtype=jnp.int32)
    weights = (positions[None, :] < sentence_len[:, None]).astype(jnp.float32)
    return jnp.sum(shaped * weights[:, :, None], axis=1) / sentence_len.astype(jnp.float32)[:, None]


def per_device(hidden_in, norm_gain, gate_weight, up_weight, down_weight, lengths):
    section_index = lax.axis_index("section")
    tick_count = MICRO + lax.axis_size("section") - 1
    gate_full, up_full, down_full = (
        lax.all_gather(gate_weight[0], "dp", axis=0, tiled=True),
        lax.all_gather(up_weight[0], "dp", axis=0, tiled=True),
        lax.all_gather(down_weight[0], "dp", axis=0, tiled=True),
    )
    gain_full = norm_gain[0]
    columns = D // lax.axis_size("tensor")
    tensor_index = lax.axis_index("tensor")

    def plan(step_index):
        micro_index = step_index - section_index
        active = jnp.logical_and(micro_index >= 0, micro_index < MICRO)
        clipped = jnp.clip(micro_index, 0, MICRO - 1)
        return (active, clipped)

    def store_unit(pooled_units, unit_rows, active, clipped):
        updated = lax.dynamic_update_slice_in_dim(pooled_units, unit_rows, clipped * SENT_MB, 0)
        return jnp.where(active, updated, pooled_units)

    source = lax.all_gather(hidden_in, "tensor", axis=1, tiled=True)

    def advance(step_index, loop_state):
        incoming, pooled_units = loop_state
        active, clipped = plan(step_index)
        entering = lax.dynamic_slice_in_dim(source, clipped * MB_TOK, MB_TOK, 0)
        current = jnp.where(section_index == 0, entering, incoming)
        wide_state = current.astype(jnp.float32)
        inv_rms = lax.rsqrt(jnp.mean(wide_state * wide_state, axis=1, keepdims=True) + RMS_EPS)
        normed = (wide_state * inv_rms * gain_full[None, :]).astype(jnp.bfloat16)
        gate_sum = jnp.dot(normed, gate_full, preferred_element_type=jnp.float32)
        up_sum = jnp.dot(normed, up_full, preferred_element_type=jnp.float32)
        hidden = (jax.nn.silu(gate_sum) * up_sum).astype(jnp.bfloat16)
        partial_value = lax.dot_general(
            hidden, down_full, CONTRACT_LAST, preferred_element_type=jnp.float32
        )
        reduced = lax.psum_scatter(
            partial_value.astype(jnp.bfloat16), "tensor", scatter_dimension=1, tiled=True
        ).astype(jnp.float32)
        residual_part = lax.dynamic_slice_in_dim(wide_state, tensor_index * columns, columns, 1)
        output_part = (residual_part + reduced).astype(jnp.bfloat16)
        output = lax.all_gather(output_part, "tensor", axis=1, tiled=True)
        sentence_len = lax.dynamic_slice_in_dim(lengths, clipped * SENT_MB, SENT_MB, 0)
        pooled = pool_rows(output, sentence_len)
        centered = pooled - jnp.mean(pooled, axis=1, keepdims=True)
        unit_rows = (
            centered * lax.rsqrt(jnp.mean(centered * centered, axis=1, keepdims=True) + UNIT_FLOOR)
        ).astype(jnp.bfloat16)
        pooled_units = store_unit(pooled_units, unit_rows, active, clipped)
        incoming = passed_along(output, "section", 1)
        return (incoming, pooled_units)

    initial = (jnp.zeros((MB_TOK, D), jnp.bfloat16), jnp.zeros((SENT_DEV, D), jnp.bfloat16))
    leftover, pooled_units = lax.fori_loop(0, tick_count, advance, initial)
    everyone = lax.all_gather(pooled_units, "dp", axis=0, tiled=True)
    products = lax.dot_general(
        pooled_units, everyone, CONTRACT_LAST, preferred_element_type=jnp.float32
    )
    return (1.0 - products / D)[None]


def solution(mesh):
    placed = (
        P("dp", "tensor"),
        P("section", None),
        P("section", "dp", "tensor"),
        P("section", "dp", "tensor"),
        P("section", "dp", "tensor"),
        P("dp"),
    )
    return jax.shard_map(
        per_device, mesh=mesh, in_specs=placed, out_specs=P("section", "dp", None), check_vma=False
    )
```

profile of v0, /device:TPU:6, one launch (start us, length us, event | category | flops | bytes accessed | tf_op | source)
XLA Modules:
  0.0 2006.2 jit_solution(17687943995972261553)
XLA Ops:
  11.0 560.5 %all-gather.8.cloned.1.call-done = bf16[1,4096,4096]{2,1,0:T(8,128)(2,1)} async-done(((bf16[1,1024,4096]{2,1,0:T(8,128)(2,1)}), bf16[1,4096,4096]{2,1,0:T(8,128)(2,1)}) %all-gather.8.cloned.1.call-update) | async-done | bytes 33554448 | tf_op jit(solution)/shard_map/all_gather | solution.py:36
  571.5 561.2 %all-gather.10.cloned.1.call-done = bf16[1,4096,4096]{2,1,0:T(8,128)(2,1)} async-done(((bf16[1,1024,4096]{2,1,0:T(8,128)(2,1)}), bf16[1,4096,4096]{2,1,0:T(8,128)(2,1)}) %all-gather.10.cloned.1.call-update) | async-done | bytes 33554448 | tf_op jit(solution)/shard_map/all_gather | solution.py:37
  1132.7 561.2 %all-gather.12.cloned.1.call-done = bf16[1,4096,4096]{2,1,0:T(8,128)(2,1)} async-done(((bf16[1,1024,4096]{2,1,0:T(8,128)(2,1)}), bf16[1,4096,4096]{2,1,0:T(8,128)(2,1)}) %all-gather.12.cloned.1.call-update) | async-done | bytes 33554448 | tf_op jit(solution)/shard_map/all_gather | solution.py:38
  1693.9 291.4 %while.17 = (s32[]{:T(128)}, bf16[16,4096]{1,0:T(8,128)(2,1)S(1)}, bf16[4,4096]{1,0:T(4,128)(2,1)S(1)}, pred[]{:T(512)}, s32[]{:T(128)}, /*index=5*/bf16[32,4096...) while((s32[]{:T(128)}, bf16[16,4096]{1,0:T(8,128)(2,1)S(1)}, ...), condition=%wide.region_6.7_spmd, body=%wide.region_0.6_spmd.sunk | while | flops 1612283904 | bytes 104368168 | solution.py:87
  1694.2 14.8 fusion.34
  1709.0 24.5 %convolution_convert_fusion.2 = bf16[16,4096]{1,0:T(8,128)(2,1)} fusion(bf16[4096,4096]{1,0:T(8,128)(2,1)} %get-tuple-element.430, bf16[4096,4096]{1,0:T(8,128)(2,1)} %get-tuple-element.429, f32[16,4096]{1,0:T(8,128)S(1)} %fusion.34, f32[4096]{0:T(1024)S(1)} %bitcast.29, f32[16]{0:T(128)S(1)} %add_rsqrt_fusion.4, ...), kind=kOutput, calls=%fused_computation.2.clone.1 | convolution fusion | flops 1074462720 | bytes 67649600 | tf_op jit(solution)/shard_map/while/body/eval_jaxpr/dot_general | solution.py:67
  1733.7 6.0 reduce-scatter.2.cloned.1.call-done
  1744.4 5.6 collective-permute-done
  1750.2 14.8 fusion.34
  1765.0 24.5 %convolution_convert_fusion.2 = bf16[16,4096]{1,0:T(8,128)(2,1)} fusion(bf16[4096,4096]{1,0:T(8,128)(2,1)} %get-tuple-element.430, bf16[4096,4096]{1,0:T(8,128)(2,1)} %get-tuple-element.429, f32[16,4096]{1,0:T(8,128)S(1)} %fusion.34, f32[4096]{0:T(1024)S(1)} %bitcast.29, f32[16]{0:T(128)S(1)} %add_rsqrt_fusion.4, ...), kind=kOutput, calls=%fused_computation.2.clone.1 | convolution fusion | flops 1074462720 | bytes 67649600 | tf_op jit(solution)/shard_map/while/body/eval_jaxpr/dot_general | solution.py:67
  1789.8 8.7 reduce-scatter.2.cloned.1.call-done
  1803.2 5.6 collective-permute-done
  1809.1 14.8 fusion.34
  1823.9 24.5 %convolution_convert_fusion.2 = bf16[16,4096]{1,0:T(8,128)(2,1)} fusion(bf16[4096,4096]{1,0:T(8,128)(2,1)} %get-tuple-element.430, bf16[4096,4096]{1,0:T(8,128)(2,1)} %get-tuple-element.429, f32[16,4096]{1,0:T(8,128)S(1)} %fusion.34, f32[4096]{0:T(1024)S(1)} %bitcast.29, f32[16]{0:T(128)S(1)} %add_rsqrt_fusion.4, ...), kind=kOutput, calls=%fused_computation.2.clone.1 | convolution fusion | flops 1074462720 | bytes 67649600 | tf_op jit(solution)/shard_map/while/body/eval_jaxpr/dot_general | solution.py:67
  1848.6 8.7 reduce-scatter.2.cloned.1.call-done
  1867.8 14.8 fusion.34
  1882.6 24.5 %convolution_convert_fusion.2 = bf16[16,4096]{1,0:T(8,128)(2,1)} fusion(bf16[4096,4096]{1,0:T(8,128)(2,1)} %get-tuple-element.430, bf16[4096,4096]{1,0:T(8,128)(2,1)} %get-tuple-element.429, f32[16,4096]{1,0:T(8,128)S(1)} %fusion.34, f32[4096]{0:T(1024)S(1)} %bitcast.29, f32[16]{0:T(128)S(1)} %add_rsqrt_fusion.4, ...), kind=kOutput, calls=%fused_computation.2.clone.1 | convolution fusion | flops 1074462720 | bytes 67649600 | tf_op jit(solution)/shard_map/while/body/eval_jaxpr/dot_general | solution.py:67
  1907.4 8.7 reduce-scatter.2.cloned.1.call-done
  1920.8 5.6 collective-permute-done
  1926.6 14.8 fusion.34
  1941.4 24.5 %convolution_convert_fusion.2 = bf16[16,4096]{1,0:T(8,128)(2,1)} fusion(bf16[4096,4096]{1,0:T(8,128)(2,1)} %get-tuple-element.430, bf16[4096,4096]{1,0:T(8,128)(2,1)} %get-tuple-element.429, f32[16,4096]{1,0:T(8,128)S(1)} %fusion.34, f32[4096]{0:T(1024)S(1)} %bitcast.29, f32[16]{0:T(128)S(1)} %add_rsqrt_fusion.4, ...), kind=kOutput, calls=%fused_computation.2.clone.1 | convolution fusion | flops 1074462720 | bytes 67649600 | tf_op jit(solution)/shard_map/while/body/eval_jaxpr/dot_general | solution.py:67
  1966.1 8.7 reduce-scatter.2.cloned.1.call-done
  1979.6 5.6 collective-permute-done
  1985.2 13.4 all-gather.3
  (112 shorter events, 36.5 us)
Async XLA Ops:
  6.5 565.0 %all-gather.8.cloned.1.call-start = ((), (), s32[]{:S(2)}) async-start(), calls=%async_computation.1 | async-start | bytes 41943040 | tf_op jit(solution)/shard_map/all_gather | solution.py:36
  7.3 1125.4 %all-gather.10.cloned.1.call-start = ((), (), s32[]{:S(2)}) async-start(), calls=%async_computation.2 | async-start | bytes 41943040 | tf_op jit(solution)/shard_map/all_gather | solution.py:37
  8.0 1685.8 %all-gather.12.cloned.1.call-start = ((), (), s32[]{:S(2)}) async-start(), calls=%async_computation.3 | async-start | bytes 41943040 | tf_op jit(solution)/shard_map/all_gather | solution.py:38
  1693.9 15.1 copy-start
  1693.9 45.8 %reduce-scatter.2.cloned.1.call-start = ((), (), s32[]{:S(2)}) async-start(), calls=%async_computation.4 | async-start | bytes 196608 | tf_op jit(solution)/shard_map/while/body/eval_jaxpr/reduce_scatter | solution.py:70
  1709.0 24.6 %copy-start.1 = (s32[4]{0:T(128)S(1)}, s32[4]{0:T(128)}, u32[]{:S(2)}) copy-start(s32[4]{0:T(128)} %get-tuple-element.431) | copy-start | bytes 52 | tf_op jit(solution)/shard_map/while
  1742.4 7.6 collective-permute-start
  1750.0 15.0 copy-start
  1750.0 48.4 %reduce-scatter.2.cloned.1.call-start = ((), (), s32[]{:S(2)}) async-start(), calls=%async_computation.4 | async-start | bytes 196608 | tf_op jit(solution)/shard_map/while/body/eval_jaxpr/reduce_scatter | solution.py:70
  1765.0 24.6 %copy-start.1 = (s32[4]{0:T(128)S(1)}, s32[4]{0:T(128)}, u32[]{:S(2)}) copy-start(s32[4]{0:T(128)} %get-tuple-element.431) | copy-start | bytes 52 | tf_op jit(solution)/shard_map/while
  1801.2 7.6 collective-permute-start
  1808.9 15.0 copy-start
  1808.9 48.4 %reduce-scatter.2.cloned.1.call-start = ((), (), s32[]{:S(2)}) async-start(), calls=%async_computation.4 | async-start | bytes 196608 | tf_op jit(solution)/shard_map/while/body/eval_jaxpr/reduce_scatter | solution.py:70
  1823.8 24.6 %copy-start.1 = (s32[4]{0:T(128)S(1)}, s32[4]{0:T(128)}, u32[]{:S(2)}) copy-start(s32[4]{0:T(128)} %get-tuple-element.431) | copy-start | bytes 52 | tf_op jit(solution)/shard_map/while
  1860.0 7.6 collective-permute-start
  1867.6 15.0 copy-start
  1867.6 48.4 %reduce-scatter.2.cloned.1.call-start = ((), (), s32[]{:S(2)}) async-start(), calls=%async_computation.4 | async-start | bytes 196608 | tf_op jit(solution)/shard_map/while/body/eval_jaxpr/reduce_scatter | solution.py:70
  1882.6 24.6 %copy-start.1 = (s32[4]{0:T(128)S(1)}, s32[4]{0:T(128)}, u32[]{:S(2)}) copy-start(s32[4]{0:T(128)} %get-tuple-element.431) | copy-start | bytes 52 | tf_op jit(solution)/shard_map/while
  1918.8 7.6 collective-permute-start
  1926.4 15.0 copy-start
  1926.4 48.4 %reduce-scatter.2.cloned.1.call-start = ((), (), s32[]{:S(2)}) async-start(), calls=%async_computation.4 | async-start | bytes 196608 | tf_op jit(solution)/shard_map/while/body/eval_jaxpr/reduce_scatter | solution.py:70
  1941.4 24.6 %copy-start.1 = (s32[4]{0:T(128)S(1)}, s32[4]{0:T(128)}, u32[]{:S(2)}) copy-start(s32[4]{0:T(128)} %get-tuple-element.431) | copy-start | bytes 52 | tf_op jit(solution)/shard_map/while
  1977.6 7.6 collective-permute-start
Sparse Core Ops, SparseCore 0:
  8.9 562.5 all-gather.7
  573.1 559.5 all-gather.9
  1134.2 559.5 all-gather.11
  1733.6 5.9 reduce-scatter.1
  1789.7 8.6 reduce-scatter.1
  1848.5 8.6 reduce-scatter.1
  1907.3 8.6 reduce-scatter.1
  1966.1 8.7 reduce-scatter.1
where the time goes:
time: 2010 us
  waiting for transfers between devices  1750 us (87%)
  matrix products  197 us (10%)
  blocking collectives  25.1 us (1%)
    all_gather x1, waiting for transfers between devices, per_device(): lax.all_gather(down_weight[0], 'dp', axis=0, tiled=True)  561 us
    all_gather x1, waiting for transfers between devices, per_device(): lax.all_gather(up_weight[0], 'dp', axis=0, tiled=True)  561 us
    all_gather x1, waiting for transfers between devices, per_device(): lax.all_gather(gate_weight[0], 'dp', axis=0, tiled=True)  561 us
    dot_general x5, matrix products, advance(): lax.dot_general(hidden, down_full, CONTRACT_LAST, preferred_element_type=...  123 us
    dot_general x5, matrix products, advance(): gate_sum = jnp.dot(normed, gate_full, preferred_element_type=jnp.float32)  74 us
    reduce_scatter x5, waiting for transfers between devices, advance(): lax.psum_scatter(partial_value.astype(jnp.bfloat16), 'tensor', scatter_di...  40.6 us
  transfers between devices with their start and end apart: 13, of which 13 were waited for; matrix products, arithmetic and copies ran while one was open for 0% of the time, Pallas kernels for 0%

commit v1 on v0

v1 whole, which is shorter than its diff:
```python
import jax
import jax.numpy as jnp
from jax import lax
from jax.sharding import PartitionSpec as P

RMS_EPS = 1e-05
UNIT_FLOOR = 0.1
CONTRACT_LAST = (((1,), (1,)), ((), ()))


def per_device(hidden_in, norm_gain, gate_weight, up_weight, down_weight, lengths):
    section = lax.axis_index("section")
    dp = lax.axis_index("dp")
    sections = lax.axis_size("section")
    dps = lax.axis_size("dp")
    gate, up, down = gate_weight[0], up_weight[0], down_weight[0]
    width = gate.shape[0]
    d_model = width * dps
    gain = lax.dynamic_slice_in_dim(norm_gain[0], dp * width, width, 0)
    source = lax.all_gather(hidden_in, "tensor", axis=1, tiled=True)
    state = lax.all_to_all(source, "dp", split_axis=1, concat_axis=0, tiled=True)
    lens = lax.all_gather(lengths, "dp", axis=0, tiled=True)
    final = state
    pairs = [(i, i + 1) for i in range(sections - 1)]
    for tick in range(sections):
        wide = state.astype(jnp.float32)
        total = lax.psum(jnp.sum(wide * wide, axis=1, keepdims=True), "dp")
        normed = (wide * lax.rsqrt(total / d_model + RMS_EPS) * gain[None, :]).astype(jnp.bfloat16)
        g = jnp.dot(normed, gate, preferred_element_type=jnp.float32).astype(jnp.bfloat16)
        u = jnp.dot(normed, up, preferred_element_type=jnp.float32).astype(jnp.bfloat16)
        both = lax.psum_scatter(jnp.concatenate([g, u], axis=1), "dp", scatter_dimension=0, tiled=True)
        both = both.astype(jnp.float32)
        cols = gate.shape[1]
        hidden = (jax.nn.silu(both[:, :cols]) * both[:, cols:]).astype(jnp.bfloat16)
        hidden = lax.all_gather(hidden, "dp", axis=0, tiled=True)
        part = lax.dot_general(hidden, down, CONTRACT_LAST, preferred_element_type=jnp.float32)
        summed = lax.psum(part.astype(jnp.bfloat16), "tensor").astype(jnp.float32)
        out = (wide + summed).astype(jnp.bfloat16)
        final = jnp.where(section == tick, out, final)
        if tick < sections - 1:
            state = lax.ppermute(out, "section", pairs)
    sents = lens.shape[0]
    shaped = final.astype(jnp.float32).reshape(sents, -1, width)
    positions = jnp.arange(shaped.shape[1], dtype=jnp.int32)
    weights = (positions[None, :] < lens[:, None]).astype(jnp.float32)
    pooled = jnp.sum(shaped * weights[:, :, None], axis=1) / lens.astype(jnp.float32)[:, None]
    mean = lax.psum(jnp.sum(pooled, axis=1, keepdims=True), "dp") / d_model
    centered = pooled - mean
    var = lax.psum(jnp.sum(centered * centered, axis=1, keepdims=True), "dp") / d_model
    unit = (centered * lax.rsqrt(var + UNIT_FLOOR)).astype(jnp.bfloat16)
    products = lax.dot_general(unit, unit, CONTRACT_LAST, preferred_element_type=jnp.float32)
    products = lax.psum_scatter(products, "dp", scatter_dimension=0, tiled=True)
    return (1.0 - products / d_model)[None]


def solution(mesh):
    placed = (
        P("dp", "tensor"),
        P("section", None),
        P("section", "dp", "tensor"),
        P("section", "dp", "tensor"),
        P("section", "dp", "tensor"),
        P("dp"),
    )
    return jax.shard_map(
        per_device, mesh=mesh, in_specs=placed, out_specs=P("section", "dp", None), check_vma=False
    )
```

time: 2010 us -> 574 us (0.29)
  waiting for transfers between devices: 1750 us -> 375 us
  matrix products: 197 us -> 63.9 us
  blocking collectives: 25.1 us -> 85.6 us
    all_gather x3 -> x4, waiting for transfers between devices: 1680 us -> 109 us  [per_device(): hidden = lax.all_gather(hidden, 'dp', axis=0, tiled=True)]
    dot_general x11 -> x13, matrix products: 197 us -> 63.9 us  [the longest x4 29.4 us: per_device(): lax.dot_general(hidden, down, CONTRACT_LAST, preferred_element_type=jnp.f...]
    reduce_scatter x5 -> x4, waiting for transfers between devices: 40.6 us -> 168 us  [per_device(): lax.psum_scatter(jnp.concatenate([g, u], axis=1), 'dp', scatter_dimension...]
    psum x0 -> x6, blocking collectives: none -> 65.1 us  [the longest x4 45 us: per_device(): total = lax.psum(jnp.sum(wide * wide, axis=1, keepdims=True), 'dp')]
    psum x0 -> x4, waiting for transfers between devices: none -> 62.1 us  [per_device(): summed = lax.psum(part.astype(jnp.bfloat16), 'tensor').astype(jnp.float32)]
    all_gather x6 -> x0, blocking collectives: 22.9 us -> none  [the longest x1 13.4 us: per_device(): everyone = lax.all_gather(pooled_units, 'dp', axis=0, tiled=True)]
  transfers between devices with their start and end apart: 13 -> 16, of which waited for: 13 -> 16; matrix products, arithmetic and copies ran while one was open for 0% -> 0% of each run, Pallas kernels for 0% -> 0%
where the time goes in v1:
time: 574 us; the launch traced here: 572 us
  waiting for transfers between devices  375 us (65%)
  blocking collectives  85.6 us (15%)
  matrix products  63.9 us (11%)
  other arithmetic  20.2 us (4%)
  between operations  15.1 us (3%)
  starting transfers between devices  9.21 us (2%)
    reduce_scatter x4, waiting for transfers between devices, per_device(): lax.psum_scatter(jnp.concatenate([g, u], axis=1), 'dp', scatter_dimension...  168 us
    all_gather x4, waiting for transfers between devices, per_device(): hidden = lax.all_gather(hidden, 'dp', axis=0, tiled=True)  109 us
    psum x4, waiting for transfers between devices, per_device(): summed = lax.psum(part.astype(jnp.bfloat16), 'tensor').astype(jnp.float32)  62.1 us
    psum x4, blocking collectives, per_device(): total = lax.psum(jnp.sum(wide * wide, axis=1, keepdims=True), 'dp')  45 us
    dot_general x4, matrix products, per_device(): lax.dot_general(hidden, down, CONTRACT_LAST, preferred_element_type=jnp.f...  29.4 us
    ppermute x3, waiting for transfers between devices, per_device(): state = lax.ppermute(out, 'section', pairs)  27.2 us
    dot_general x4, matrix products, per_device(): jnp.dot(normed, gate, preferred_element_type=jnp.float32)  18.9 us
    unnamed x2, blocking collectives  18.2 us
  transfers between devices with their start and end apart: 16, of which 16 were waited for; matrix products, arithmetic and copies ran while one was open for 0% of the time, Pallas kernels for 0%

profile of v1, /device:TPU:6, one launch (start us, length us, event | category | flops | bytes accessed | tf_op | source)
XLA Modules:
  0.0 571.9 jit_solution(8479298247538401880)
XLA Ops:
  14.5 9.2 %all-to-all-done = bf16[32,4,1024]{2,0,1:T(8,128)(2,1)S(1)} async-done(((bf16[32,4,1024]{2,0,1:T(8,128)(2,1)}), bf16[32,4,1024]{2,0,1:T(8,128)(2,1)S(1)}, u32[]{:S(2)}, u32[]{:S(2)}) %all-to-all-start) | async-done | bytes 262176 | tf_op jit(solution)/shard_map/all_to_all | solution.py:21
  23.9 9.8 %psum.70 = f32[128,1]{0,1:T(1,128)S(1)} all-reduce(f32[128,1]{0,1:T(1,128)S(1)} %broadcast_in_dim.14), channel_id=1, replica_groups=mesh['section'=4,'tensor'=2,'dp'=4] {'dp'}, use_global_device_ids=true, to_apply=%region_1.0 | all-reduce | flops 128 | bytes 1024 | tf_op jit(solution)/shard_map/psum | solution.py:27
  42.4 41.9 %reduce-scatter.5.cloned.1.call-done = bf16[32,8192]{1,0:T(8,128)(2,1)} async-done(((bf16[128,8192]{1,0:T(8,128)(2,1)}), bf16[32,8192]{1,0:T(8,128)(2,1)}) %reduce-scatter.5.cloned.1.call-update) | async-done | bytes 524304 | tf_op jit(solution)/shard_map/reduce_scatter | solution.py:31
  86.4 27.3 %all-gather.5.cloned.1.call-done = bf16[128,4096]{1,0:T(8,128)(2,1)} async-done(((bf16[32,4096]{1,0:T(8,128)(2,1)}), bf16[128,4096]{1,0:T(8,128)(2,1)}) %all-gather.5.cloned.1.call-update) | async-done | bytes 1048592 | tf_op jit(solution)/shard_map/all_gather | solution.py:35
  121.1 18.0 %all-reduce.7.cloned.1.call-done = bf16[128,1024]{1,0:T(8,128)(2,1)} async-done(((bf16[128,1024]{1,0:T(8,128)(2,1)}), bf16[128,1024]{1,0:T(8,128)(2,1)}) %all-reduce.7.cloned.1.call-update) | async-done | bytes 262160 | tf_op jit(solution)/shard_map/psum | solution.py:37
  141.4 9.1 %collective-permute-done = bf16[128,1024]{1,0:T(8,128)(2,1)S(1)} collective-permute-done((bf16[128,1024]{1,0:T(8,128)(2,1)S(1)}, bf16[128,1024]{1,0:T(8,128)(2,1)S(1)}, u32[]{:S(2)}, u32[]{:S(2)}) %collective-permute-start) | collective-permute-done | bytes 262176 | tf_op jit(solution)/shard_map/ppermute | solution.py:41
  150.6 11.7 %psum.72 = f32[128,1]{0,1:T(1,128)S(1)} all-reduce(f32[128,1]{0,1:T(1,128)S(1)} %bitcast.112), channel_id=1, replica_groups=mesh['section'=4,'tensor'=2,'dp'=4] {'dp'}, use_global_device_ids=true, to_apply=%region_5.6 | all-reduce | flops 128 | bytes 1024 | tf_op jit(solution)/shard_map/psum | solution.py:27
  173.3 41.9 %reduce-scatter.7.cloned.1.call-done = bf16[32,8192]{1,0:T(8,128)(2,1)} async-done(((bf16[128,8192]{1,0:T(8,128)(2,1)}), bf16[32,8192]{1,0:T(8,128)(2,1)}) %reduce-scatter.7.cloned.1.call-update) | async-done | bytes 524304 | tf_op jit(solution)/shard_map/reduce_scatter | solution.py:31
  217.2 27.3 %all-gather.7.cloned.1.call-done = bf16[128,4096]{1,0:T(8,128)(2,1)} async-done(((bf16[32,4096]{1,0:T(8,128)(2,1)}), bf16[128,4096]{1,0:T(8,128)(2,1)}) %all-gather.7.cloned.1.call-update) | async-done | bytes 1048592 | tf_op jit(solution)/shard_map/all_gather | solution.py:35
  251.9 18.0 %all-reduce.9.cloned.1.call-done = bf16[128,1024]{1,0:T(8,128)(2,1)} async-done(((bf16[128,1024]{1,0:T(8,128)(2,1)}), bf16[128,1024]{1,0:T(8,128)(2,1)}) %all-reduce.9.cloned.1.call-update) | async-done | bytes 262160 | tf_op jit(solution)/shard_map/psum | solution.py:37
  272.3 9.1 %collective-permute-done.1 = bf16[128,1024]{1,0:T(8,128)(2,1)S(1)} collective-permute-done((bf16[128,1024]{1,0:T(8,128)(2,1)S(1)}, bf16[128,1024]{1,0:T(8,128)(2,1)S(1)}, u32[]{:S(2)}, u32[]{:S(2)}) %collective-permute-start.1) | collective-permute-done | bytes 262176 | tf_op jit(solution)/shard_map/ppermute | solution.py:41
  281.5 11.9 %psum.74 = f32[128,1]{0,1:T(1,128)S(1)} all-reduce(f32[128,1]{0,1:T(1,128)S(1)} %bitcast.113), channel_id=1, replica_groups=mesh['section'=4,'tensor'=2,'dp'=4] {'dp'}, use_global_device_ids=true, to_apply=%region_9.10 | all-reduce | flops 128 | bytes 1024 | tf_op jit(solution)/shard_map/psum | solution.py:27
  304.4 41.9 %reduce-scatter.9.cloned.1.call-done = bf16[32,8192]{1,0:T(8,128)(2,1)} async-done(((bf16[128,8192]{1,0:T(8,128)(2,1)}), bf16[32,8192]{1,0:T(8,128)(2,1)}) %reduce-scatter.9.cloned.1.call-update) | async-done | bytes 524304 | tf_op jit(solution)/shard_map/reduce_scatter | solution.py:31
  348.3 27.3 %all-gather.9.cloned.1.call-done = bf16[128,4096]{1,0:T(8,128)(2,1)} async-done(((bf16[32,4096]{1,0:T(8,128)(2,1)}), bf16[128,4096]{1,0:T(8,128)(2,1)}) %all-gather.9.cloned.1.call-update) | async-done | bytes 1048592 | tf_op jit(solution)/shard_map/all_gather | solution.py:35
  383.0 18.0 %all-reduce.11.cloned.1.call-done = bf16[128,1024]{1,0:T(8,128)(2,1)} async-done(((bf16[128,1024]{1,0:T(8,128)(2,1)}), bf16[128,1024]{1,0:T(8,128)(2,1)}) %all-reduce.11.cloned.1.call-update) | async-done | bytes 262160 | tf_op jit(solution)/shard_map/psum | solution.py:37
  403.3 9.1 %collective-permute-done.2 = bf16[128,1024]{1,0:T(8,128)(2,1)S(1)} collective-permute-done((bf16[128,1024]{1,0:T(8,128)(2,1)S(1)}, bf16[128,1024]{1,0:T(8,128)(2,1)S(1)}, u32[]{:S(2)}, u32[]{:S(2)}) %collective-permute-start.2) | collective-permute-done | bytes 262176 | tf_op jit(solution)/shard_map/ppermute | solution.py:41
  412.5 11.7 %psum.76 = f32[128,1]{0,1:T(1,128)S(1)} all-reduce(f32[128,1]{0,1:T(1,128)S(1)} %bitcast.114), channel_id=1, replica_groups=mesh['section'=4,'tensor'=2,'dp'=4] {'dp'}, use_global_device_ids=true, to_apply=%region_13.14 | all-reduce | flops 128 | bytes 1024 | tf_op jit(solution)/shard_map/psum | solution.py:27
  435.3 41.9 %reduce-scatter.11.cloned.1.call-done = bf16[32,8192]{1,0:T(8,128)(2,1)} async-done(((bf16[128,8192]{1,0:T(8,128)(2,1)}), bf16[32,8192]{1,0:T(8,128)(2,1)}) %reduce-scatter.11.cloned.1.call-update) | async-done | bytes 524304 | tf_op jit(solution)/shard_map/reduce_scatter | solution.py:31
  479.2 27.3 %all-gather.11.cloned.1.call-done = bf16[128,4096]{1,0:T(8,128)(2,1)} async-done(((bf16[32,4096]{1,0:T(8,128)(2,1)}), bf16[128,4096]{1,0:T(8,128)(2,1)}) %all-gather.11.cloned.1.call-update) | async-done | bytes 1048592 | tf_op jit(solution)/shard_map/all_gather | solution.py:35
  515.4 7.7 %all-reduce = s32[16]{0:T(128)S(1)} all-reduce(s32[16]{0:T(128)S(1)} %dynamic-update-slice), channel_id=1, replica_groups=mesh['section'=4,'tensor'=2,'dp'=4] {'dp'}, use_global_device_ids=true, to_apply=%add | all-reduce | flops 16 | bytes 128
  523.8 8.1 %all-reduce.13.cloned.1.call-done = bf16[128,1024]{1,0:T(8,128)(2,1)} async-done(((bf16[128,1024]{1,0:T(8,128)(2,1)}), bf16[128,1024]{1,0:T(8,128)(2,1)}) %all-reduce.13.cloned.1.call-update) | async-done | bytes 262160 | tf_op jit(solution)/shard_map/psum | solution.py:37
  533.5 11.7 %psum.78 = f32[16,1]{0,1:T(1,128)S(1)} all-reduce(f32[16,1]{0,1:T(1,128)S(1)} %bitcast.115), channel_id=1, replica_groups=mesh['section'=4,'tensor'=2,'dp'=4] {'dp'}, use_global_device_ids=true, to_apply=%region_18.19 | all-reduce | flops 16 | bytes 128 | tf_op jit(solution)/shard_map/psum | solution.py:47
  545.4 8.4 %psum.79 = f32[16,1]{0,1:T(1,128)S(1)} all-reduce(f32[16,1]{0,1:T(1,128)S(1)} %bitcast.116), channel_id=1, replica_groups=mesh['section'=4,'tensor'=2,'dp'=4] {'dp'}, use_global_device_ids=true, to_apply=%region_20.21 | all-reduce | flops 16 | bytes 128 | tf_op jit(solution)/shard_map/psum | solution.py:49
  554.0 10.5 %all-reduce.1 = f32[16,16]{1,0:T(8,128)S(1)} all-reduce(f32[16,16]{1,0:T(8,128)S(1)} %fusion.90), channel_id=6, replica_groups=mesh['section'=4,'tensor'=2,'dp'=4] {'dp'}, use_global_device_ids=true, to_apply=%region_21.22.clone | all-reduce | flops 256 | bytes 2048
  (91 shorter events, 98.4 us)
Async XLA Ops:
  6.5 7.9 %copy-start = (f32[1,4096]{1,0:T(1,128)S(1)}, f32[1,4096]{1,0:T(1,128)}, u32[]{:S(2)}) copy-start(f32[1,4096]{1,0:T(1,128)} %param.7) | copy-start | bytes 49156
  9.6 14.1 %all-to-all-start = ((bf16[32,4,1024]{2,0,1:T(8,128)(2,1)}), bf16[32,4,1024]{2,0,1:T(8,128)(2,1)S(1)}, u32[]{:S(2)}, u32[]{:S(2)}) async-start(bf16[32,4,1024]{2,0,1:T(8,128)(2,1)} %bitcast.101), calls=%async_computation | async-start | bytes 524288 | tf_op jit(solution)/shard_map/all_to_all | solution.py:21
  14.4 69.9 %reduce-scatter.5.cloned.1.call-start = ((), (), s32[]{:S(2)}) async-start(), calls=%async_computation.5 | async-start | bytes 2621440 | tf_op jit(solution)/shard_map/reduce_scatter | solution.py:31
  33.8 5.8 %copy-start.1 = (bf16[1,1024,4096]{2,1,0:T(8,128)(2,1)S(1)}, bf16[1,1024,4096]{2,1,0:T(8,128)(2,1)}, u32[]{:S(2)}) copy-start(bf16[1,1024,4096]{2,1,0:T(8,128)(2,1)} %param.9) | copy-start | bytes 25165828
  42.3 71.3 %all-gather.5.cloned.1.call-start = ((), (), s32[]{:S(2)}) async-start(), calls=%async_computation.6 | async-start | bytes 1310720 | tf_op jit(solution)/shard_map/all_gather | solution.py:35
  86.3 52.7 %all-reduce.7.cloned.1.call-start = ((), (), s32[]{:S(2)}) async-start(), calls=%async_computation.7 | async-start | bytes 524288 | tf_op jit(solution)/shard_map/psum | solution.py:37
  121.0 94.1 %reduce-scatter.7.cloned.1.call-start = ((), (), s32[]{:S(2)}) async-start(), calls=%async_computation.8 | async-start | bytes 2621440 | tf_op jit(solution)/shard_map/reduce_scatter | solution.py:31
  140.1 10.4 %collective-permute-start = (bf16[128,1024]{1,0:T(8,128)(2,1)S(1)}, bf16[128,1024]{1,0:T(8,128)(2,1)S(1)}, u32[]{:S(2)}, u32[]{:S(2)}) collective-permute-start(bf16[128,1024]{1,0:T(8,128)(2,1)S(1)} %add_convert_fusion), channel_id=1, source_target_pairs={{0,8},{8,16},{16,24},{1,9},{9,17},{17,25},{2,10},{10,18},{18,26},{... | collective-permute-start | bytes 786440 | tf_op jit(solution)/shard_map/ppermute | solution.py:41
  173.2 71.3 %all-gather.7.cloned.1.call-start = ((), (), s32[]{:S(2)}) async-start(), calls=%async_computation.9 | async-start | bytes 1310720 | tf_op jit(solution)/shard_map/all_gather | solution.py:35
  217.2 52.8 %all-reduce.9.cloned.1.call-start = ((), (), s32[]{:S(2)}) async-start(), calls=%async_computation.10 | async-start | bytes 524288 | tf_op jit(solution)/shard_map/psum | solution.py:37
  251.9 94.3 %reduce-scatter.9.cloned.1.call-start = ((), (), s32[]{:S(2)}) async-start(), calls=%async_computation.11 | async-start | bytes 2621440 | tf_op jit(solution)/shard_map/reduce_scatter | solution.py:31
  271.0 10.4 %collective-permute-start.1 = (bf16[128,1024]{1,0:T(8,128)(2,1)S(1)}, bf16[128,1024]{1,0:T(8,128)(2,1)S(1)}, u32[]{:S(2)}, u32[]{:S(2)}) collective-permute-start(bf16[128,1024]{1,0:T(8,128)(2,1)S(1)} %fusion.66), channel_id=1, source_target_pairs={{0,8},{8,16},{16,24},{1,9},{9,17},{17,25},{2,10},{10,18},{18,26},{... | collective-permute-start | bytes 786440 | tf_op jit(solution)/shard_map/ppermute | solution.py:41
  304.3 71.3 %all-gather.9.cloned.1.call-start = ((), (), s32[]{:S(2)}) async-start(), calls=%async_computation.12 | async-start | bytes 1310720 | tf_op jit(solution)/shard_map/all_gather | solution.py:35
  348.2 52.8 %all-reduce.11.cloned.1.call-start = ((), (), s32[]{:S(2)}) async-start(), calls=%async_computation.13 | async-start | bytes 524288 | tf_op jit(solution)/shard_map/psum | solution.py:37
  382.9 94.2 %reduce-scatter.11.cloned.1.call-start = ((), (), s32[]{:S(2)}) async-start(), calls=%async_computation.14 | async-start | bytes 2621440 | tf_op jit(solution)/shard_map/reduce_scatter | solution.py:31
  402.0 10.4 %collective-permute-start.2 = (bf16[128,1024]{1,0:T(8,128)(2,1)S(1)}, bf16[128,1024]{1,0:T(8,128)(2,1)S(1)}, u32[]{:S(2)}, u32[]{:S(2)}) collective-permute-start(bf16[128,1024]{1,0:T(8,128)(2,1)S(1)} %fusion.70), channel_id=1, source_target_pairs={{0,8},{8,16},{16,24},{1,9},{9,17},{17,25},{2,10},{10,18},{18,26},{... | collective-permute-start | bytes 786440 | tf_op jit(solution)/shard_map/ppermute | solution.py:41
  435.2 78.7 %copy-start.3 = (u32[32]{0:T(128)S(1)}, u32[32]{0:T(128)}, u32[]{:S(2)}) copy-start(u32[32]{0:T(128)} %constant.50) | copy-start | bytes 388
  435.2 80.0 %copy-start.4 = (s32[4]{0:T(128)S(1)}, s32[4]{0:T(128)}, u32[]{:S(2)}) copy-start(s32[4]{0:T(128)} %param.11) | copy-start | bytes 52
  435.2 96.7 %copy-start.2 = (bf16[128,1024]{1,0:T(8,128)(2,1)S(1)}, bf16[128,1024]{1,0:T(8,128)(2,1)}, u32[]{:S(2)}) copy-start(bf16[128,1024]{1,0:T(8,128)(2,1)} %all-reduce.7.cloned.1.call-done) | copy-start | bytes 786436
  435.2 71.3 %all-gather.11.cloned.1.call-start = ((), (), s32[]{:S(2)}) async-start(), calls=%async_computation.15 | async-start | bytes 1310720 | tf_op jit(solution)/shard_map/all_gather | solution.py:35
  479.2 52.7 %all-reduce.13.cloned.1.call-start = ((), (), s32[]{:S(2)}) async-start(), calls=%async_computation.16 | async-start | bytes 524288 | tf_op jit(solution)/shard_map/psum | solution.py:37
Sparse Core Ops, SparseCore 0:
  42.5 41.8 reduce-scatter.4
  86.4 27.1 all-gather.4
  121.1 17.8 all-reduce.6
  173.4 41.7 reduce-scatter.6
  217.3 27.1 all-gather.6
  252.0 17.8 all-reduce.8
  304.4 41.7 reduce-scatter.8
  348.3 27.1 all-gather.8
  383.1 17.8 all-reduce.10
  435.3 41.7 reduce-scatter.10
  479.3 27.1 all-gather.10
  514.0 17.8 all-reduce.12

commit v2 on v1

v2 whole, which is shorter than its diff:
```python
import functools

import jax
import jax.numpy as jnp
from jax import lax
from jax.experimental import pallas as pl
from jax.experimental.pallas import tpu as pltpu
from jax.sharding import PartitionSpec as P

RMS_EPS = 1e-05
UNIT_FLOOR = 0.1
CONTRACT_LAST = (((1,), (1,)), ((), ()))
MESH = pl.DeviceIdType.MESH
LANES = 128
F32 = jnp.float32
BF16 = jnp.bfloat16


def kernel(dps, tensors, sections, hidden_ref, gain_ref, mask_ref, lens_ref, gate_hbm, up_hbm, down_hbm,
           out_ref, gate_v, up_v, down_v, x_in, rs_out, rs_in, own_gu, own_ss, hid, tx, outs, stat, gram,
           w_sem, d_send, x_send, x_recv, rs_send, rs_recv, h_send, h_recv, t_send, t_recv,
           s_send, s_recv, g_send, g_recv):
    section = lax.axis_index("section")
    tensor = lax.axis_index("tensor")
    dp = lax.axis_index("dp")
    micros = dps
    width = gate_v.shape[0]
    cols = gate_v.shape[1]
    fc = cols // dps
    rows = x_in.shape[1]
    d_model = width * dps
    nj = hidden_ref.shape[1] // width

    def chunk(c):
        return pl.ds(pl.multiple_of(c * fc, fc), fc)

    def wcopy(which, c):
        src, dst = ((gate_hbm, gate_v), (up_hbm, up_v), (down_hbm, down_v))[which]
        return pltpu.make_async_copy(src.at[0, :, chunk(c)], dst.at[:, chunk(c)], w_sem.at[which, c])

    order = [lax.rem(dp + k, dps) for k in range(1, dps + 1)]
    for c in order:
        wcopy(0, c).start()
        wcopy(1, c).start()
    for c in order:
        wcopy(2, c).start()

    barrier = pltpu.get_barrier_semaphore()
    for kt in range(tensors):
        for kd in range(dps):
            if kt or kd:
                pl.semaphore_signal(
                    barrier, inc=1,
                    device_id={"tensor": lax.rem(tensor + kt, tensors), "dp": lax.rem(dp + kd, dps)},
                    device_id_type=MESH)

    @pl.when(section > 0)
    def _():
        pl.semaphore_signal(barrier, inc=1, device_id={"section": section - 1}, device_id_type=MESH)

    @pl.when(section < sections - 1)
    def _():
        pl.semaphore_signal(barrier, inc=1, device_id={"section": section + 1}, device_id_type=MESH)

    pl.semaphore_wait(
        barrier,
        tensors * dps + 1 - jnp.where(section == 0, 1, 0) - jnp.where(section == sections - 1, 1, 0))

    def spread(j, k):
        return pltpu.make_async_remote_copy(
            src_ref=hidden_ref.at[:, pl.ds(j * width, width)], dst_ref=x_in.at[dp],
            send_sem=d_send.at[j, k], recv_sem=x_recv.at[dp],
            device_id={"tensor": lax.rem(tensor + k, tensors), "dp": tensor * nj + j}, device_id_type=MESH)

    @pl.when(section == 0)
    def _():
        for j in range(nj):
            for k in range(tensors):
                if k:
                    spread(j, k).start()
                else:
                    @pl.when(tensor * nj + j != dp)
                    def _():
                        spread(j, k).start()

                    @pl.when(tensor * nj + j == dp)
                    def _():
                        x_in[dp] = hidden_ref[:, j * width:(j + 1) * width]

    def rs_copy(m, c):
        return pltpu.make_async_remote_copy(
            src_ref=rs_out.at[m, c], dst_ref=rs_in.at[m, dp],
            send_sem=rs_send.at[m, c], recv_sem=rs_recv.at[m, dp],
            device_id={"dp": c}, device_id_type=MESH)

    def rs_wait(m, c):
        return pltpu.make_async_remote_copy(
            src_ref=rs_out.at[m, c], dst_ref=rs_in.at[m, c],
            send_sem=rs_send.at[m, c], recv_sem=rs_recv.at[m, c],
            device_id={"dp": c}, device_id_type=MESH)

    def h_copy(m, c, peer):
        return pltpu.make_async_remote_copy(
            src_ref=hid.at[m, c], dst_ref=hid.at[m, c],
            send_sem=h_send.at[m, peer], recv_sem=h_recv.at[m, c],
            device_id={"dp": peer}, device_id_type=MESH)

    def t_copy(m, c, peer):
        return pltpu.make_async_remote_copy(
            src_ref=tx.at[m, c], dst_ref=tx.at[m, c],
            send_sem=t_send.at[m, peer], recv_sem=t_recv.at[m, c],
            device_id={"tensor": peer}, device_id_type=MESH)

    def x_copy(m, to):
        return pltpu.make_async_remote_copy(
            src_ref=outs.at[m], dst_ref=x_in.at[m],
            send_sem=x_send.at[m], recv_sem=x_recv.at[m],
            device_id={"section": to}, device_id_type=MESH)

    lane = lax.broadcasted_iota(jnp.int32, (rows, LANES), 1)

    def gate_up(m):
        local = jnp.logical_and(section == 0, jnp.logical_and(m == dp, lax.div(dp, nj) == tensor))

        @pl.when(jnp.logical_not(local))
        def _():
            x_copy(m, section).wait_recv()

        x = x_in[m].astype(F32)
        ss = jnp.sum(x * x, axis=1, keepdims=True)
        high = ss.astype(BF16)
        low = (ss - high.astype(F32)).astype(BF16)
        packed = jnp.where(lane < LANES // 2, high.astype(F32), low.astype(F32)).astype(BF16)
        own_ss[m] = jnp.broadcast_to(ss, (rows, LANES))
        scaled = (x * gain_ref[...]).astype(BF16)
        for k in range(1, dps + 1):
            c = lax.rem(dp + k, dps)

            @pl.when(m == 0)
            def _():
                wcopy(0, c).wait()
                wcopy(1, c).wait()

            g = jnp.dot(scaled, gate_v[:, chunk(c)], preferred_element_type=F32)
            u = jnp.dot(scaled, up_v[:, chunk(c)], preferred_element_type=F32)
            if k < dps:
                rs_out[m, c, :, 0:fc] = g.astype(BF16)
                rs_out[m, c, :, fc:2 * fc] = u.astype(BF16)
                rs_out[m, c, :, 2 * fc:] = packed
                rs_copy(m, c).start()
            else:
                own_gu[m, :, 0:fc] = g
                own_gu[m, :, fc:] = u

    def activate(m):
        for k in range(1, dps):
            rs_wait(m, lax.rem(dp + k, dps)).wait_recv()
        g = own_gu[m, :, 0:fc]
        u = own_gu[m, :, fc:]
        ss = own_ss[m][:, 0:1]
        for k in range(1, dps):
            c = lax.rem(dp + k, dps)
            g = g + rs_in[m, c, :, 0:fc].astype(F32)
            u = u + rs_in[m, c, :, fc:2 * fc].astype(F32)
            ss = ss + jnp.sum(rs_in[m, c, :, 2 * fc:].astype(F32), axis=1, keepdims=True) * (2.0 / LANES)
        inv = lax.rsqrt(ss * (1.0 / d_model) + RMS_EPS)
        g = g * inv
        u = u * inv
        hid[m, dp] = (g / (1.0 + jnp.exp(-g)) * u).astype(BF16)
        for k in range(1, dps):
            h_copy(m, dp, lax.rem(dp + k, dps)).start()

    def finish(m):
        acc = jnp.zeros((rows, width), F32)
        for k in range(dps):
            c = lax.rem(dp + k, dps)
            if k:
                h_copy(m, c, c).wait_recv()

            @pl.when(m == 0)
            def _():
                wcopy(2, c).wait()

            acc = acc + lax.dot_general(hid[m, c], down_v[:, chunk(c)], CONTRACT_LAST,
                                        preferred_element_type=F32)
        tx[m, tensor] = acc.astype(BF16)
        for k in range(1, tensors):
            t_copy(m, tensor, lax.rem(tensor + k, tensors)).start()
        for k in range(1, tensors):
            other = lax.rem(tensor + k, tensors)
            t_copy(m, other, other).wait_recv()
        total = tx[m, 0].astype(F32)
        for t in range(1, tensors):
            total = total + tx[m, t].astype(F32)
        outs[m] = (x_in[m].astype(F32) + total).astype(BF16)

        @pl.when(section < sections - 1)
        def _():
            x_copy(m, section + 1).start()

    def step(m, carry):
        gate_up(m)
        activate(m)
        finish(m)
        return carry

    lax.fori_loop(0, micros, step, 0)

    sents = mask_ref.shape[0]
    pooled = jnp.zeros((sents, width), F32)
    for m in range(micros):
        pooled = pooled + jnp.dot(mask_ref[:, m * rows:(m + 1) * rows], outs[m], preferred_element_type=F32)
    pooled = pooled / lens_ref[:, 0:1]

    def s_copy(buf, send, recv, c, peer):
        return pltpu.make_async_remote_copy(
            src_ref=buf.at[c], dst_ref=buf.at[c], send_sem=send.at[peer], recv_sem=recv.at[c],
            device_id={"dp": peer}, device_id_type=MESH)

    def share(buf, send, recv):
        for k in range(1, dps):
            s_copy(buf, send, recv, dp, lax.rem(dp + k, dps)).start()
        for k in range(1, dps):
            c = lax.rem(dp + k, dps)
            s_copy(buf, send, recv, c, c).wait_recv()

    stat[dp] = jnp.broadcast_to(jnp.sum(pooled, axis=1, keepdims=True), (sents, LANES))
    share(stat, s_send, s_recv)
    total = stat[0]
    for c in range(1, dps):
        total = total + stat[c]
    centered = pooled - total[:, 0:1] * (1.0 / d_model)
    narrow = centered.astype(BF16)
    sq = jnp.sum(centered * centered, axis=1, keepdims=True)
    gram[dp, 0] = jnp.zeros((sents, LANES), F32)
    gram[dp, 0, :, 0:sents] = lax.dot_general(narrow, narrow, CONTRACT_LAST, preferred_element_type=F32)
    gram[dp, 1] = jnp.broadcast_to(sq, (sents, LANES))
    share(gram, g_send, g_recv)
    products = gram[0, 0]
    sq = gram[0, 1]
    for c in range(1, dps):
        products = products + gram[c, 0]
        sq = sq + gram[c, 1]
    scale = lax.rsqrt(sq * (1.0 / d_model) + UNIT_FLOOR)
    r_i = lax.broadcasted_iota(jnp.int32, (sents, LANES), 0)
    c_i = lax.broadcasted_iota(jnp.int32, (sents, LANES), 1)
    across = jnp.sum(jnp.where(r_i == c_i, scale, 0.0), axis=0, keepdims=True)
    out_ref[...] = 1.0 - products * scale * across * (1.0 / d_model)

    @pl.when(section == 0)
    def _():
        for j in range(nj):
            for k in range(tensors):
                if k:
                    spread(j, k).wait_send()
                else:
                    @pl.when(tensor * nj + j != dp)
                    def _():
                        spread(j, k).wait_send()

    def drain(m, carry):
        for k in range(1, dps):
            c = lax.rem(dp + k, dps)
            rs_copy(m, c).wait_send()
            h_copy(m, dp, c).wait_send()
        for k in range(1, tensors):
            t_copy(m, tensor, lax.rem(tensor + k, tensors)).wait_send()

        @pl.when(section < sections - 1)
        def _():
            x_copy(m, section + 1).wait_send()
        return carry

    lax.fori_loop(0, micros, drain, 0)
    for k in range(1, dps):
        c = lax.rem(dp + k, dps)
        s_copy(stat, s_send, s_recv, dp, c).wait_send()
        s_copy(gram, g_send, g_recv, dp, c).wait_send()


def per_device(hidden_in, norm_gain, gate_weight, up_weight, down_weight, lengths):
    dp = lax.axis_index("dp")
    sections = lax.axis_size("section")
    tensors = lax.axis_size("tensor")
    dps = lax.axis_size("dp")
    _, width, cols = gate_weight.shape
    rows = hidden_in.shape[0]
    fc = cols // dps
    nj = hidden_in.shape[1] // width
    gain = lax.dynamic_slice_in_dim(norm_gain, dp * width, width, 1)
    lens = lax.all_gather(lengths, "dp", axis=0, tiled=True)
    sents = lens.shape[0]
    per = rows * dps // sents
    token = jnp.arange(rows * dps, dtype=jnp.int32)[None, :] - per * jnp.arange(sents, dtype=jnp.int32)[:, None]
    mask = jnp.logical_and(token >= 0, token < lens[:, None]).astype(BF16)
    lens_wide = jnp.broadcast_to(lens.astype(F32)[:, None], (sents, LANES))
    vm = pl.BlockSpec(memory_space=pltpu.VMEM)
    hbm = pl.BlockSpec(memory_space=pl.ANY)
    dma = pltpu.SemaphoreType.DMA
    result = pl.pallas_call(
        functools.partial(kernel, dps, tensors, sections),
        out_shape=jax.ShapeDtypeStruct((sents, LANES), F32),
        in_specs=[vm] * 4 + [hbm] * 3,
        out_specs=vm,
        scratch_shapes=[
            pltpu.VMEM((width, cols), BF16),
            pltpu.VMEM((width, cols), BF16),
            pltpu.VMEM((width, cols), BF16),
            pltpu.VMEM((dps, rows, width), BF16),
            pltpu.VMEM((dps, dps, rows, 2 * fc + LANES), BF16),
            pltpu.VMEM((dps, dps, rows, 2 * fc + LANES), BF16),
            pltpu.VMEM((dps, rows, 2 * fc), F32),
            pltpu.VMEM((dps, rows, LANES), F32),
            pltpu.VMEM((dps, dps, rows, fc), BF16),
            pltpu.VMEM((dps, tensors, rows, width), BF16),
            pltpu.VMEM((dps, rows, width), BF16),
            pltpu.VMEM((dps, sents, LANES), F32),
            pltpu.VMEM((dps, 2, sents, LANES), F32),
            dma((3, dps)),
            dma((nj, tensors)),
            dma((dps,)),
            dma((dps,)),
            dma((dps, dps)),
            dma((dps, dps)),
            dma((dps, dps)),
            dma((dps, dps)),
            dma((dps, tensors)),
            dma((dps, tensors)),
            dma((dps,)),
            dma((dps,)),
            dma((dps,)),
            dma((dps,)),
        ],
        compiler_params=pltpu.CompilerParams(
            collective_id=0, has_side_effects=True, vmem_limit_bytes=60 * 1024 * 1024),
    )(hidden_in, gain, mask, lens_wide, gate_weight, up_weight, down_weight)
    each = sents // dps
    return lax.dynamic_slice_in_dim(result, dp * each, each, 0)[None, :, :sents]


def solution(mesh):
    placed = (
        P("dp", "tensor"),
        P("section", None),
        P("section", "dp", "tensor"),
        P("section", "dp", "tensor"),
        P("section", "dp", "tensor"),
        P("dp"),
    )
    return jax.shard_map(
        per_device, mesh=mesh, in_specs=placed, out_specs=P("section", "dp", None), check_vma=False
    )
```

time: 574 us -> 212 us (0.37)
  waiting for transfers between devices: 375 us -> 0 us
  Pallas kernels: 0 us -> 198 us
  blocking collectives: 85.6 us -> 8.44 us
  matrix products: 63.9 us -> 0 us
  other arithmetic: 20.2 us -> 0.68 us
  between operations: 15.1 us -> 0.67 us
  starting transfers between devices: 9.21 us -> 0 us
    pallas_call x0 -> x1, Pallas kernels: none -> 198 us  [per_device(): pl.pallas_call(functools.partial(kernel, dps, tensors, sections), out_sha...]
    reduce_scatter x4 -> x0, waiting for transfers between devices: 168 us -> none  [per_device(): lax.psum_scatter(jnp.concatenate([g, u], axis=1), 'dp', scatter_dimension...]
    all_gather x4 -> x0, waiting for transfers between devices: 109 us -> none  [per_device(): hidden = lax.all_gather(hidden, 'dp', axis=0, tiled=True)]
    psum x6 -> x0, blocking collectives: 65.1 us -> none  [the longest x4 45 us: per_device(): total = lax.psum(jnp.sum(wide * wide, axis=1, keepdims=True), 'dp')]
    dot_general x13 -> x0, matrix products: 63.9 us -> none  [the longest x4 29.4 us: per_device(): lax.dot_general(hidden, down, CONTRACT_LAST, preferred_element_type=jnp.f...]
    psum x4 -> x0, waiting for transfers between devices: 62.1 us -> none  [per_device(): summed = lax.psum(part.astype(jnp.bfloat16), 'tensor').astype(jnp.float32)]
    ppermute x3 -> x0, waiting for transfers between devices: 27.2 us -> none  [per_device(): state = lax.ppermute(out, 'section', pairs)]
    convert_element_type x14 -> x2, other arithmetic: 11.2 us -> 0.68 us  [the longest x1 0.67 us: per_device(): mask = jnp.logical_and(token >= 0, token < lens[:, None]).astype(BF16)]
  transfers between devices with their start and end apart: 16 -> 0, of which waited for: 16 -> 0; matrix products, arithmetic and copies ran while one was open for 0% -> 0% of each run, Pallas kernels for 0% -> 0%
where the time goes in v2:
time: 212 us
  Pallas kernels  198 us (93%)
  blocking collectives  8.44 us (4%)
  local copies, waits for them, and re-layouts  4.63 us (2%)
    pallas_call x1, Pallas kernels, per_device(): pl.pallas_call(functools.partial(kernel, dps, tensors, sections), out_sha...  198 us
    unnamed x1, blocking collectives  8.44 us

profile of v2, /device:TPU:6, one launch (start us, length us, event | category | flops | bytes accessed | tf_op | source)
XLA Modules:
  0.0 212.1 jit_solution(17449391240166410264)
XLA Ops:
  0.0 0.0 copy-start
  0.0 1.2 dynamic-slice
  1.9 0.9 dynamic-update-slice
  2.8 8.4 %all-reduce = s32[16]{0:T(128)S(1)} all-reduce(s32[16]{0:T(128)S(1)} %dynamic-update-slice), channel_id=1, replica_groups=mesh['section'=4,'tensor'=2,'dp'=4] {'dp'}, use_global_device_ids=true, to_apply=%add | all-reduce | flops 16 | bytes 128
  11.2 0.7 fusion.3.mask_ref
  11.9 0.0 copy-done
  11.9 0.6 constant_dynamic-slice_fusion.1.gain_ref
  12.5 0.7 broadcast_in_dim.4.lens_ref
  13.2 197.6 %shard_map.64 = f32[16,128]{1,0:T(8,128)} custom-call(bf16[32,2048]{1,0:T(8,128)(2,1)} %hidden_ref.1, f32[1,1024]{1,0:T(1,128)} %constant_dynamic-slice_fusion.1.gain_ref, bf16[16,128]{1,0:T(8,128)(2,1)} %fusion.3.mask_ref, f32[16,128]{1,0:T(8,128)} %broadcast_in_dim.4.lens_ref, bf16[1,1024,4096]{2,1,0:T(8,128)(2,1)} %gate_hbm.1, ...), custom_call_target="tpu_custom_call" | custom-call | tf_op jit(solution)/shard_map/pallas_call | solution.py:300
  210.8 0.7 constant_dynamic-slice_fusion
  211.5 0.6 slice_bitcast_fusion
  (3 shorter events, 0.0 us)
Async XLA Ops:
  0.0 11.9 %copy-start = (f32[1,4096]{1,0:T(1,128)S(1)}, f32[1,4096]{1,0:T(1,128)}, u32[]{:S(2)}) copy-start(f32[1,4096]{1,0:T(1,128)} %param.7) | copy-start | bytes 49156

commit v3 on v2

v3 whole, which is shorter than its diff:
```python
import functools

import jax
import jax.numpy as jnp
from jax import lax
from jax.experimental import pallas as pl
from jax.experimental.pallas import tpu as pltpu
from jax.sharding import PartitionSpec as P

RMS_EPS = 1e-05
UNIT_FLOOR = 0.1
CONTRACT_LAST = (((1,), (1,)), ((), ()))
MESH = pl.DeviceIdType.MESH
LANES = 128
F32 = jnp.float32
BF16 = jnp.bfloat16


SPLIT = 2


def kernel(dps, tensors, sections, hidden_ref, gain_ref, lens_ref, gate_hbm, up_hbm, down_hbm,
           out_ref, gate_v, up_v, down_v, x_in, rs_out, rs_in, own_gu, own_ss, hid, tx, outs, stat, gram, lbuf, lens_full,
           w_sem, d_send, x_send, x_recv, rs_send, rs_recv, h_send, h_recv, t_send, t_recv,
           s_send, s_recv, g_send, g_recv, l_send, l_recv):
    section = lax.axis_index("section")
    tensor = lax.axis_index("tensor")
    dp = lax.axis_index("dp")
    micros = dps * SPLIT
    width = gate_v.shape[0]
    cols = gate_v.shape[1]
    fc = cols // dps
    rows = x_in.shape[1]
    d_model = width * dps
    nj = hidden_ref.shape[1] // width

    def chunk(c):
        return pl.ds(pl.multiple_of(c * fc, fc), fc)

    def wcopy(which, c):
        src, dst = ((gate_hbm, gate_v), (up_hbm, up_v), (down_hbm, down_v))[which]
        return pltpu.make_async_copy(src.at[0, :, chunk(c)], dst.at[:, chunk(c)], w_sem.at[which, c])

    if dps == 4:
        mirror = dps - 1 - dp
        peers = [mirror, lax.rem(dp + 2, dps), lax.rem(mirror + 2, dps)]
    else:
        peers = [lax.rem(dp + k, dps) for k in range(1, dps)]
    order = peers + [dp]
    for c in order:
        wcopy(0, c).start()
        wcopy(1, c).start()
    for c in order:
        wcopy(2, c).start()

    barrier = pltpu.get_barrier_semaphore()
    for kt in range(tensors):
        for kd in range(dps):
            if kt or kd:
                pl.semaphore_signal(
                    barrier, inc=1,
                    device_id={"tensor": lax.rem(tensor + kt, tensors), "dp": lax.rem(dp + kd, dps)},
                    device_id_type=MESH)

    @pl.when(section > 0)
    def _():
        pl.semaphore_signal(barrier, inc=1, device_id={"section": section - 1}, device_id_type=MESH)

    @pl.when(section < sections - 1)
    def _():
        pl.semaphore_signal(barrier, inc=1, device_id={"section": section + 1}, device_id_type=MESH)

    pl.semaphore_wait(
        barrier,
        tensors * dps + 1 - jnp.where(section == 0, 1, 0) - jnp.where(section == sections - 1, 1, 0))

    each = lens_ref.shape[0]
    sents = each * dps
    slot = lax.broadcasted_iota(jnp.int32, lbuf.shape[1:], 0)
    own_lens = jnp.ones(lbuf.shape[1:], F32)
    for n in range(each):
        own_lens = jnp.where(slot == n, lens_ref[n].astype(F32), own_lens)
    lbuf[dp] = own_lens

    def s_copy(buf, send, recv, c, peer):
        return pltpu.make_async_remote_copy(
            src_ref=buf.at[c], dst_ref=buf.at[c], send_sem=send.at[peer], recv_sem=recv.at[c],
            device_id={"dp": peer}, device_id_type=MESH)

    def spread(h, j, k):
        return pltpu.make_async_remote_copy(
            src_ref=hidden_ref.at[pl.ds(h * rows, rows), pl.ds(j * width, width)],
            dst_ref=x_in.at[dp * SPLIT + h],
            send_sem=d_send.at[h, j * tensors + k], recv_sem=x_recv.at[dp * SPLIT + h],
            device_id={"tensor": lax.rem(tensor + k, tensors), "dp": tensor * nj + j}, device_id_type=MESH)

    @pl.when(section == 0)
    def _():
        for h in range(SPLIT):
            for j in range(nj):
                for k in range(tensors):
                    if k:
                        spread(h, j, k).start()
                    else:
                        @pl.when(tensor * nj + j != dp)
                        def _():
                            spread(h, j, k).start()

                        @pl.when(tensor * nj + j == dp)
                        def _():
                            x_in[dp * SPLIT + h] = hidden_ref[h * rows:(h + 1) * rows, j * width:(j + 1) * width]

    for c in peers:
        s_copy(lbuf, l_send, l_recv, dp, c).start()

    def rs_copy(m, c):
        return pltpu.make_async_remote_copy(
            src_ref=rs_out.at[m, c], dst_ref=rs_in.at[m, dp],
            send_sem=rs_send.at[m, c], recv_sem=rs_recv.at[m, dp],
            device_id={"dp": c}, device_id_type=MESH)

    def rs_wait(m, c):
        return pltpu.make_async_remote_copy(
            src_ref=rs_out.at[m, c], dst_ref=rs_in.at[m, c],
            send_sem=rs_send.at[m, c], recv_sem=rs_recv.at[m, c],
            device_id={"dp": c}, device_id_type=MESH)

    def h_copy(m, c, peer):
        return pltpu.make_async_remote_copy(
            src_ref=hid.at[m, c], dst_ref=hid.at[m, c],
            send_sem=h_send.at[m, peer], recv_sem=h_recv.at[m, c],
            device_id={"dp": peer}, device_id_type=MESH)

    def t_copy(m, c, peer):
        return pltpu.make_async_remote_copy(
            src_ref=tx.at[m, c], dst_ref=tx.at[m, c],
            send_sem=t_send.at[m, peer], recv_sem=t_recv.at[m, c],
            device_id={"tensor": peer}, device_id_type=MESH)

    def x_copy(m, to):
        return pltpu.make_async_remote_copy(
            src_ref=outs.at[m], dst_ref=x_in.at[m],
            send_sem=x_send.at[m], recv_sem=x_recv.at[m],
            device_id={"section": to}, device_id_type=MESH)

    lane = lax.broadcasted_iota(jnp.int32, (rows, LANES), 1)

    def gate_up(m):
        local = jnp.logical_and(section == 0, jnp.logical_and(m // SPLIT == dp, dp // nj == tensor))

        @pl.when(jnp.logical_not(local))
        def _():
            x_copy(m, section).wait_recv()

        x = x_in[m].astype(F32)
        ss = jnp.sum(x * x, axis=1, keepdims=True)
        high = ss.astype(BF16)
        low = (ss - high.astype(F32)).astype(BF16)
        packed = jnp.where(lane < LANES // 2, high.astype(F32), low.astype(F32)).astype(BF16)
        own_ss[m] = jnp.broadcast_to(ss, (rows, LANES))
        scaled = (x * gain_ref[:, pl.ds(pl.multiple_of(dp * width, width), width)]).astype(BF16)
        for k, c in enumerate(order):
            @pl.when(m == 0)
            def _():
                wcopy(0, c).wait()
                wcopy(1, c).wait()

            g = jnp.dot(scaled, gate_v[:, chunk(c)], preferred_element_type=F32)
            u = jnp.dot(scaled, up_v[:, chunk(c)], preferred_element_type=F32)
            if k < dps - 1:
                rs_out[m, c, :, 0:fc] = g.astype(BF16)
                rs_out[m, c, :, fc:2 * fc] = u.astype(BF16)
                rs_out[m, c, :, 2 * fc:] = packed
                rs_copy(m, c).start()
            else:
                own_gu[m, :, 0:fc] = g
                own_gu[m, :, fc:] = u

    def activate(m):
        for c in peers:
            rs_wait(m, c).wait_recv()
        g = own_gu[m, :, 0:fc]
        u = own_gu[m, :, fc:]
        ss = own_ss[m][:, 0:1]
        for c in peers:
            g = g + rs_in[m, c, :, 0:fc].astype(F32)
            u = u + rs_in[m, c, :, fc:2 * fc].astype(F32)
            ss = ss + jnp.sum(rs_in[m, c, :, 2 * fc:].astype(F32), axis=1, keepdims=True) * (2.0 / LANES)
        inv = lax.rsqrt(ss * (1.0 / d_model) + RMS_EPS)
        g = g * inv
        u = u * inv
        hid[m, dp] = (g / (1.0 + jnp.exp(-g)) * u).astype(BF16)
        for c in peers:
            h_copy(m, dp, c).start()

    def finish(m):
        acc = jnp.zeros((rows, width), F32)
        for k, c in enumerate([dp] + peers[::2] + peers[1::2]):
            if k:
                h_copy(m, c, c).wait_recv()

            @pl.when(m == 0)
            def _():
                wcopy(2, c).wait()

            acc = acc + lax.dot_general(hid[m, c], down_v[:, chunk(c)], CONTRACT_LAST,
                                        preferred_element_type=F32)
        tx[m, tensor] = acc.astype(BF16)
        for k in range(1, tensors):
            t_copy(m, tensor, lax.rem(tensor + k, tensors)).start()
        for k in range(1, tensors):
            other = lax.rem(tensor + k, tensors)
            t_copy(m, other, other).wait_recv()
        total = tx[m, 0].astype(F32)
        for t in range(1, tensors):
            total = total + tx[m, t].astype(F32)
        outs[m] = (x_in[m].astype(F32) + total).astype(BF16)

        @pl.when(section < sections - 1)
        def _():
            x_copy(m, section + 1).start()

    def step(i, carry):
        @pl.when(i < micros)
        def _():
            gate_up(i)

        @pl.when(i > 0)
        def _():
            finish(i - 1)

        @pl.when(i < micros)
        def _():
            activate(i)
        return carry

    lax.fori_loop(0, micros + 1, step, 0)

    for c in peers:
        s_copy(lbuf, l_send, l_recv, c, c).wait_recv()
    for c in range(dps):
        lens_full[c * each:(c + 1) * each] = lbuf[c, 0:each]
    tokens = micros * rows
    per = tokens // sents
    place = lax.broadcasted_iota(jnp.int32, (sents, tokens), 1) - per * lax.broadcasted_iota(
        jnp.int32, (sents, tokens), 0)
    lens = lens_full[:, 0:1]
    valid = jnp.logical_and(place >= 0, place.astype(F32) < lens)
    mask = jnp.where(valid, 1.0, 0.0).astype(BF16)
    pooled = jnp.dot(mask, outs[...].reshape(tokens, width), preferred_element_type=F32) / lens

    def share(buf, send, recv):
        for c in peers:
            s_copy(buf, send, recv, dp, c).start()
        for c in peers:
            s_copy(buf, send, recv, c, c).wait_recv()

    stat[dp] = jnp.broadcast_to(jnp.sum(pooled, axis=1, keepdims=True), (sents, LANES))
    share(stat, s_send, s_recv)
    total = stat[0]
    for c in range(1, dps):
        total = total + stat[c]
    centered = pooled - total[:, 0:1] * (1.0 / d_model)
    narrow = centered.astype(BF16)
    sq = jnp.sum(centered * centered, axis=1, keepdims=True)
    gram[dp, 0] = jnp.zeros((sents, LANES), F32)
    gram[dp, 0, :, 0:sents] = lax.dot_general(narrow, narrow, CONTRACT_LAST, preferred_element_type=F32)
    gram[dp, 1] = jnp.broadcast_to(sq, (sents, LANES))
    share(gram, g_send, g_recv)
    products = gram[0, 0]
    sq = gram[0, 1]
    for c in range(1, dps):
        products = products + gram[c, 0]
        sq = sq + gram[c, 1]
    scale = lax.rsqrt(sq * (1.0 / d_model) + UNIT_FLOOR)
    r_i = lax.broadcasted_iota(jnp.int32, (sents, LANES), 0)
    c_i = lax.broadcasted_iota(jnp.int32, (sents, LANES), 1)
    across = jnp.sum(jnp.where(r_i == c_i, scale, 0.0), axis=0, keepdims=True)
    whole = 1.0 - products * scale * across * (1.0 / d_model)
    for r in range(each):
        row = jnp.sum(jnp.where(r_i == dp * each + r, whole, 0.0), axis=0, keepdims=True)
        out_ref[0, r:r + 1, :] = row[:, 0:sents]

    @pl.when(section == 0)
    def _():
        for h in range(SPLIT):
            for j in range(nj):
                for k in range(tensors):
                    if k:
                        spread(h, j, k).wait_send()
                    else:
                        @pl.when(tensor * nj + j != dp)
                        def _():
                            spread(h, j, k).wait_send()

    def drain(m, carry):
        for c in peers:
            rs_copy(m, c).wait_send()
            h_copy(m, dp, c).wait_send()
        for k in range(1, tensors):
            t_copy(m, tensor, lax.rem(tensor + k, tensors)).wait_send()

        @pl.when(section < sections - 1)
        def _():
            x_copy(m, section + 1).wait_send()
        return carry

    lax.fori_loop(0, micros, drain, 0)
    for c in peers:
        s_copy(lbuf, l_send, l_recv, dp, c).wait_send()
        s_copy(stat, s_send, s_recv, dp, c).wait_send()
        s_copy(gram, g_send, g_recv, dp, c).wait_send()


def per_device(hidden_in, norm_gain, gate_weight, up_weight, down_weight, lengths):
    sections = lax.axis_size("section")
    tensors = lax.axis_size("tensor")
    dps = lax.axis_size("dp")
    _, width, cols = gate_weight.shape
    micros = dps * SPLIT
    rows = hidden_in.shape[0] // SPLIT
    fc = cols // dps
    nj = hidden_in.shape[1] // width
    each = lengths.shape[0]
    sents = each * dps
    vm = pl.BlockSpec(memory_space=pltpu.VMEM)
    hbm = pl.BlockSpec(memory_space=pl.ANY)
    dma = pltpu.SemaphoreType.DMA
    smem = pl.BlockSpec(memory_space=pltpu.SMEM)
    return pl.pallas_call(
        functools.partial(kernel, dps, tensors, sections),
        out_shape=jax.ShapeDtypeStruct((1, each, sents), F32),
        in_specs=[vm] * 2 + [smem] + [hbm] * 3,
        out_specs=vm,
        scratch_shapes=[
            pltpu.VMEM((width, cols), BF16),
            pltpu.VMEM((width, cols), BF16),
            pltpu.VMEM((width, cols), BF16),
            pltpu.VMEM((micros, rows, width), BF16),
            pltpu.VMEM((micros, dps, rows, 2 * fc + LANES), BF16),
            pltpu.VMEM((micros, dps, rows, 2 * fc + LANES), BF16),
            pltpu.VMEM((micros, rows, 2 * fc), F32),
            pltpu.VMEM((micros, rows, LANES), F32),
            pltpu.VMEM((micros, dps, rows, fc), BF16),
            pltpu.VMEM((micros, tensors, rows, width), BF16),
            pltpu.VMEM((micros, rows, width), BF16),
            pltpu.VMEM((dps, sents, LANES), F32),
            pltpu.VMEM((dps, 2, sents, LANES), F32),
            pltpu.VMEM((dps, -(-each // 8) * 8, LANES), F32),
            pltpu.VMEM((sents, LANES), F32),
            dma((3, dps)),
            dma((SPLIT, nj * tensors)),
            dma((micros,)),
            dma((micros,)),
            dma((micros, dps)),
            dma((micros, dps)),
            dma((micros, dps)),
            dma((micros, dps)),
            dma((micros, tensors)),
            dma((micros, tensors)),
            dma((dps,)),
            dma((dps,)),
            dma((dps,)),
            dma((dps,)),
            dma((dps,)),
            dma((dps,)),
        ],
        compiler_params=pltpu.CompilerParams(
            collective_id=0, has_side_effects=True, vmem_limit_bytes=60 * 1024 * 1024),
    )(hidden_in, norm_gain, lengths, gate_weight, up_weight, down_weight)


def solution(mesh):
    placed = (
        P("dp", "tensor"),
        P("section", None),
        P("section", "dp", "tensor"),
        P("section", "dp", "tensor"),
        P("section", "dp", "tensor"),
        P("dp"),
    )
    return jax.shard_map(
        per_device, mesh=mesh, in_specs=placed, out_specs=P("section", "dp", None), check_vma=False
    )
```

time: 212 us -> 168 us (0.79)
  Pallas kernels: 198 us -> 166 us
  blocking collectives: 8.44 us -> 0 us
  local copies, waits for them, and re-layouts: 4.63 us -> 1.26 us
    pallas_call x1, Pallas kernels: 198 us -> 166 us  [per_device(): pl.pallas_call(functools.partial(kernel, dps, tensors, sections), out_sha...]
    unnamed x1 -> x0, blocking collectives: 8.44 us -> none
where the time goes in v3:
time: 168 us
  Pallas kernels  166 us (99%)
    pallas_call x1, Pallas kernels, per_device(): pl.pallas_call(functools.partial(kernel, dps, tensors, sections), out_sha...  166 us

profile of v3, /device:TPU:6, one launch (start us, length us, event | category | flops | bytes accessed | tf_op | source)
XLA Modules:
  0.0 167.7 jit_solution(14919410840156223315)
XLA Ops:
  0.0 166.4 %shard_map.64 = f32[1,4,16]{2,1,0:T(4,128)} custom-call(bf16[32,2048]{1,0:T(8,128)(2,1)} %hidden_ref.1, f32[1,4096]{1,0:T(1,128)} %gain_ref.1, s32[4]{0:T(128)} %lens_ref.1, bf16[1,1024,4096]{2,1,0:T(8,128)(2,1)} %gate_hbm.1, bf16[1,1024,4096]{2,1,0:T(8,128)(2,1)} %up_hbm.1, bf16[1,1024,4096]{2,1,0:T(8,128)(2,1)} %down_hbm.1), custom_call_target="tpu_custom_call" | custom-call | tf_op jit(solution)/shard_map/pallas_call | solution.py:330
  166.4 1.3 copy.8

commit v4 on v3

--- a/solution.py
+++ b/solution.py
@@ -19,10 +19,14 @@
 SPLIT = 2
 
 
+def pieces(fc):
+    return 2 if fc % (2 * LANES) == 0 else 1
+
+
 def kernel(dps, tensors, sections, hidden_ref, gain_ref, lens_ref, gate_hbm, up_hbm, down_hbm,
-           out_ref, gate_v, up_v, down_v, x_in, rs_out, rs_in, own_gu, own_ss, hid, tx, outs, stat, gram, lbuf, lens_full,
+           out_ref, gate_v, up_v, down_v, x_in, rs_out, rs_in, own_gu, own_ss, hid, tx, outs, gram, lbuf, lens_full,
            w_sem, d_send, x_send, x_recv, rs_send, rs_recv, h_send, h_recv, t_send, t_recv,
-           s_send, s_recv, g_send, g_recv, l_send, l_recv):
+           g_send, g_recv, l_send, l_recv):
     section = lax.axis_index("section")
     tensor = lax.axis_index("tensor")
     dp = lax.axis_index("dp")
@@ -30,6 +34,8 @@
     width = gate_v.shape[0]
     cols = gate_v.shape[1]
     fc = cols // dps
+    halves = pieces(fc)
+    fh = fc // halves
     rows = x_in.shape[1]
     d_model = width * dps
     nj = hidden_ref.shape[1] // width
@@ -113,23 +119,33 @@
     for c in peers:
         s_copy(lbuf, l_send, l_recv, dp, c).start()
 
-    def rs_copy(m, c):
-        return pltpu.make_async_remote_copy(
-            src_ref=rs_out.at[m, c], dst_ref=rs_in.at[m, dp],
-            send_sem=rs_send.at[m, c], recv_sem=rs_recv.at[m, dp],
+    def base(q):
+        return LANES + 2 * fh * q
+
+    def piece(q):
+        return pl.ds(0, base(1)) if q == 0 else pl.ds(base(q), 2 * fh)
+
+    def rs_copy(m, c, q):
+        return pltpu.make_async_remote_copy(
+            src_ref=rs_out.at[m, c, :, piece(q)], dst_ref=rs_in.at[m, dp, :, piece(q)],
+            send_sem=rs_send.at[m, c * halves + q], recv_sem=rs_recv.at[m, dp * halves + q],
             device_id={"dp": c}, device_id_type=MESH)
 
-    def rs_wait(m, c):
-        return pltpu.make_async_remote_copy(
-            src_ref=rs_out.at[m, c], dst_ref=rs_in.at[m, c],
-            send_sem=rs_send.at[m, c], recv_sem=rs_recv.at[m, c],
+    def rs_wait(m, c, q):
+        return pltpu.make_async_remote_copy(
+            src_ref=rs_out.at[m, c, :, piece(q)], dst_ref=rs_in.at[m, c, :, piece(q)],
+            send_sem=rs_send.at[m, c * halves + q], recv_sem=rs_recv.at[m, c * halves + q],
             device_id={"dp": c}, device_id_type=MESH)
 
-    def h_copy(m, c, peer):
-        return pltpu.make_async_remote_copy(
-            src_ref=hid.at[m, c], dst_ref=hid.at[m, c],
-            send_sem=h_send.at[m, peer], recv_sem=h_recv.at[m, c],
+    def h_copy(m, c, peer, q):
+        part = hid.at[m, c, :, pl.ds(q * fh, fh)]
+        return pltpu.make_async_remote_copy(
+            src_ref=part, dst_ref=part,
+            send_sem=h_send.at[m, peer * halves + q], recv_sem=h_recv.at[m, c * halves + q],
             device_id={"dp": peer}, device_id_type=MESH)
+
+    def columns(c, q):
+        return pl.ds(pl.multiple_of(c * fc + q * fh, fh), fh)
 
     def t_copy(m, c, peer):
         return pltpu.make_async_remote_copy(
@@ -159,52 +175,62 @@
         packed = jnp.where(lane < LANES // 2, high.astype(F32), low.astype(F32)).astype(BF16)
         own_ss[m] = jnp.broadcast_to(ss, (rows, LANES))
         scaled = (x * gain_ref[:, pl.ds(pl.multiple_of(dp * width, width), width)]).astype(BF16)
-        for k, c in enumerate(order):
-            @pl.when(m == 0)
-            def _():
-                wcopy(0, c).wait()
-                wcopy(1, c).wait()
-
-            g = jnp.dot(scaled, gate_v[:, chunk(c)], preferred_element_type=F32)
-            u = jnp.dot(scaled, up_v[:, chunk(c)], preferred_element_type=F32)
-            if k < dps - 1:
-                rs_out[m, c, :, 0:fc] = g.astype(BF16)
-                rs_out[m, c, :, fc:2 * fc] = u.astype(BF16)
-                rs_out[m, c, :, 2 * fc:] = packed
-                rs_copy(m, c).start()
+        for c, q in [(c, q) for q in range(halves) for c in peers] + [(dp, q) for q in range(halves)]:
+            if q == 0:
+                @pl.when(m == 0)
+                def _():
+                    wcopy(0, c).wait()
+                    wcopy(1, c).wait()
+
+            g = jnp.dot(scaled, gate_v[:, columns(c, q)], preferred_element_type=F32)
+            u = jnp.dot(scaled, up_v[:, columns(c, q)], preferred_element_type=F32)
+            at = base(q)
+            if c is not dp:
+                if q == 0:
+                    rs_out[m, c, :, 0:LANES] = packed
+                rs_out[m, c, :, at:at + fh] = g.astype(BF16)
+                rs_out[m, c, :, at + fh:at + 2 * fh] = u.astype(BF16)
+                rs_copy(m, c, q).start()
             else:
-                own_gu[m, :, 0:fc] = g
-                own_gu[m, :, fc:] = u
+                own_gu[m, :, q * 2 * fh:q * 2 * fh + fh] = g
+                own_gu[m, :, q * 2 * fh + fh:(q + 1) * 2 * fh] = u
 
     def activate(m):
-        for c in peers:
-            rs_wait(m, c).wait_recv()
-        g = own_gu[m, :, 0:fc]
-        u = own_gu[m, :, fc:]
-        ss = own_ss[m][:, 0:1]
-        for c in peers:
-            g = g + rs_in[m, c, :, 0:fc].astype(F32)
-            u = u + rs_in[m, c, :, fc:2 * fc].astype(F32)
-            ss = ss + jnp.sum(rs_in[m, c, :, 2 * fc:].astype(F32), axis=1, keepdims=True) * (2.0 / LANES)
-        inv = lax.rsqrt(ss * (1.0 / d_model) + RMS_EPS)
-        g = g * inv
-        u = u * inv
-        hid[m, dp] = (g / (1.0 + jnp.exp(-g)) * u).astype(BF16)
-        for c in peers:
-            h_copy(m, dp, c).start()
+        inv = None
+        for q in range(halves):
+            for c in peers:
+                rs_wait(m, c, q).wait_recv()
+            if q == 0:
+                ss = own_ss[m][:, 0:1]
+                for c in peers:
+                    ss = ss + jnp.sum(rs_in[m, c, :, 0:LANES].astype(F32), axis=1, keepdims=True) * (2.0 / LANES)
+                inv = lax.rsqrt(ss * (1.0 / d_model) + RMS_EPS)
+            g = own_gu[m, :, q * 2 * fh:q * 2 * fh + fh]
+            u = own_gu[m, :, q * 2 * fh + fh:(q + 1) * 2 * fh]
+            at = base(q)
+            for c in peers:
+                g = g + rs_in[m, c, :, at:at + fh].astype(F32)
+                u = u + rs_in[m, c, :, at + fh:at + 2 * fh].astype(F32)
+            g = g * inv
+            u = u * inv
+            hid[m, dp, :, q * fh:(q + 1) * fh] = (g / (1.0 + jnp.exp(-g)) * u).astype(BF16)
+            for c in peers:
+                h_copy(m, dp, c, q).start()
 
     def finish(m):
         acc = jnp.zeros((rows, width), F32)
-        for k, c in enumerate([dp] + peers[::2] + peers[1::2]):
-            if k:
-                h_copy(m, c, c).wait_recv()
-
-            @pl.when(m == 0)
-            def _():
-                wcopy(2, c).wait()
-
-            acc = acc + lax.dot_general(hid[m, c], down_v[:, chunk(c)], CONTRACT_LAST,
-                                        preferred_element_type=F32)
+        arrivals = [(dp, q) for q in range(halves)]
+        arrivals += [(c, q) for q in range(halves) for c in peers[::2] + peers[1::2]]
+        for c, q in arrivals:
+            if c is not dp:
+                h_copy(m, c, c, q).wait_recv()
+            if q == 0:
+                @pl.when(m == 0)
+                def _():
+                    wcopy(2, c).wait()
+
+            acc = acc + lax.dot_general(hid[m, c, :, q * fh:(q + 1) * fh], down_v[:, columns(c, q)],
+                                        CONTRACT_LAST, preferred_element_type=F32)
         tx[m, tensor] = acc.astype(BF16)
         for k in range(1, tensors):
             t_copy(m, tensor, lax.rem(tensor + k, tensors)).start()
@@ -255,26 +281,29 @@
         for c in peers:
             s_copy(buf, send, recv, c, c).wait_recv()
 
-    stat[dp] = jnp.broadcast_to(jnp.sum(pooled, axis=1, keepdims=True), (sents, LANES))
-    share(stat, s_send, s_recv)
-    total = stat[0]
-    for c in range(1, dps):
-        total = total + stat[c]
-    centered = pooled - total[:, 0:1] * (1.0 / d_model)
+    mean = jnp.sum(pooled, axis=1, keepdims=True) * (1.0 / width)
+    centered = pooled - mean
     narrow = centered.astype(BF16)
     sq = jnp.sum(centered * centered, axis=1, keepdims=True)
     gram[dp, 0] = jnp.zeros((sents, LANES), F32)
     gram[dp, 0, :, 0:sents] = lax.dot_general(narrow, narrow, CONTRACT_LAST, preferred_element_type=F32)
     gram[dp, 1] = jnp.broadcast_to(sq, (sents, LANES))
+    gram[dp, 2] = jnp.broadcast_to(mean, (sents, LANES))
     share(gram, g_send, g_recv)
-    products = gram[0, 0]
-    sq = gram[0, 1]
+    products, sq, mean = gram[0, 0], gram[0, 1], gram[0, 2]
     for c in range(1, dps):
         products = products + gram[c, 0]
         sq = sq + gram[c, 1]
-    scale = lax.rsqrt(sq * (1.0 / d_model) + UNIT_FLOOR)
+        mean = mean + gram[c, 2]
+    mean = mean * (1.0 / dps)
     r_i = lax.broadcasted_iota(jnp.int32, (sents, LANES), 0)
     c_i = lax.broadcasted_iota(jnp.int32, (sents, LANES), 1)
+    for c in range(dps):
+        off = gram[c, 2] - mean
+        off_row = jnp.sum(jnp.where(r_i == c_i, off, 0.0), axis=0, keepdims=True)
+        products = products + off * off_row * float(width)
+        sq = sq + off * off * float(width)
+    scale = lax.rsqrt(sq * (1.0 / d_model) + UNIT_FLOOR)
     across = jnp.sum(jnp.where(r_i == c_i, scale, 0.0), axis=0, keepdims=True)
     whole = 1.0 - products * scale * across * (1.0 / d_model)
     for r in range(each):
@@ -295,8 +324,9 @@
 
     def drain(m, carry):
         for c in peers:
-            rs_copy(m, c).wait_send()
-            h_copy(m, dp, c).wait_send()
+            for q in range(halves):
+                rs_copy(m, c, q).wait_send()
+                h_copy(m, dp, c, q).wait_send()
         for k in range(1, tensors):
             t_copy(m, tensor, lax.rem(tensor + k, tensors)).wait_send()
 
@@ -308,7 +338,6 @@
     lax.fori_loop(0, micros, drain, 0)
     for c in peers:
         s_copy(lbuf, l_send, l_recv, dp, c).wait_send()
-        s_copy(stat, s_send, s_recv, dp, c).wait_send()
         s_copy(gram, g_send, g_recv, dp, c).wait_send()
 
 
@@ -320,6 +349,7 @@
     micros = dps * SPLIT
     rows = hidden_in.shape[0] // SPLIT
     fc = cols // dps
+    halves = pieces(fc)
     nj = hidden_in.shape[1] // width
     each = lengths.shape[0]
     sents = each * dps
@@ -344,22 +374,19 @@
             pltpu.VMEM((micros, dps, rows, fc), BF16),
             pltpu.VMEM((micros, tensors, rows, width), BF16),
             pltpu.VMEM((micros, rows, width), BF16),
-            pltpu.VMEM((dps, sents, LANES), F32),
-            pltpu.VMEM((dps, 2, sents, LANES), F32),
+            pltpu.VMEM((dps, 3, sents, LANES), F32),
             pltpu.VMEM((dps, -(-each // 8) * 8, LANES), F32),
             pltpu.VMEM((sents, LANES), F32),
             dma((3, dps)),
             dma((SPLIT, nj * tensors)),
             dma((micros,)),
             dma((micros,)),
-            dma((micros, dps)),
-            dma((micros, dps)),
-            dma((micros, dps)),
-            dma((micros, dps)),
+            dma((micros, dps * halves)),
+            dma((micros, dps * halves)),
+            dma((micros, dps * halves)),
+            dma((micros, dps * halves)),
             dma((micros, tensors)),
             dma((micros, tensors)),
-            dma((dps,)),
-            dma((dps,)),
             dma((dps,)),
             dma((dps,)),
             dma((dps,)),

time: 168 us -> 152 us (0.905)
  Pallas kernels: 166 us -> 150 us
    pallas_call x1, Pallas kernels: 166 us -> 150 us  [per_device(): pl.pallas_call(functools.partial(kernel, dps, tensors, sections), out_sha...]
where the time goes in v4:
time: 152 us; the launch traced here: 151 us
  Pallas kernels  150 us (99%)
    pallas_call x1, Pallas kernels, per_device(): pl.pallas_call(functools.partial(kernel, dps, tensors, sections), out_sha...  150 us

profile of v4, /device:TPU:6, one launch (start us, length us, event | category | flops | bytes accessed | tf_op | source)
XLA Modules:
  0.0 151.0 jit_solution(12221841907211932651)
XLA Ops:
  0.0 149.7 %shard_map.64 = f32[1,4,16]{2,1,0:T(4,128)} custom-call(bf16[32,2048]{1,0:T(8,128)(2,1)} %hidden_ref.1, f32[1,4096]{1,0:T(1,128)} %gain_ref.1, s32[4]{0:T(128)} %lens_ref.1, bf16[1,1024,4096]{2,1,0:T(8,128)(2,1)} %gate_hbm.1, bf16[1,1024,4096]{2,1,0:T(8,128)(2,1)} %up_hbm.1, bf16[1,1024,4096]{2,1,0:T(8,128)(2,1)} %down_hbm.1), custom_call_target="tpu_custom_call" | custom-call | tf_op jit(solution)/shard_map/pallas_call | solution.py:360
  149.7 1.3 copy.8
